TPU v7x, 32 devices: a whole 2x2x4 slice. The times are simulated.
32 devices in a mesh: seq: 8 (over z, y), head: 4 (over x, core).
Axes of the slice: x: 2, y: 2, z: 4, core: 2. Of those that a mesh axis runs over, the one named last changes fastest.
Arguments:
- hidden_states: bfloat16 [2048, 1536], P('seq', 'head'), may hold values from -60 to 60
- feature_q: bfloat16 [1536, 384], P(None, 'head'), may hold values from -0.15625 to 0.15625
- feature_k: bfloat16 [1536, 384], P(None, 'head'), may hold values from -0.15625 to 0.15625
- value_w: bfloat16 [1536, 1536], P(None, 'head'), may hold values from -0.15625 to 0.15625
- window_q: bfloat16 [1536, 1536], P(None, 'head'), may hold values from -0.15625 to 0.15625
- window_k: bfloat16 [1536, 1536], P(None, 'head'), may hold values from -0.15625 to 0.15625
- norm_gain: float32 [1536], P('head'), may hold values from 0.5 to 1.5
Outputs:
- mixed: bfloat16 [2048, 1536], P('seq', 'head')
All inputs are finite; a program needn't handle non-finite values.
Results may differ from a plain program's by a relative error of at most 0.007.
Values may be sent and summed in bfloat16 or wider, within the bound.
A program may use at most 128 MiB of HBM per device.

v0:
```python
import jax
import jax.numpy as jnp
import numpy as np
from jax import lax
from jax.sharding import PartitionSpec as P

FK = 16
HV = 64
WINDOW_HEAD_SIZE = 64
WIN = 64
HIGH_ACCURACY = lax.Precision.HIGHEST


def from_behind(shard, axis, by):
    devices = lax.axis_size(axis)
    pairs = [(i, i + by) for i in range(devices) if 0 <= i + by < devices]
    return lax.ppermute(shard, axis, pairs)


def prefix_2(value, axis, join, neutral):
    count, mine = (lax.axis_size(axis), lax.axis_index(axis))
    pieces = lax.all_gather(value, axis)
    so_far = jnp.full_like(value, 0) + jnp.asarray(neutral, value.dtype)

    def lap(position, so_far):
        longer = join(so_far, pieces[position])
        return jnp.where(position < mine, longer, so_far)

    return lax.fori_loop(0, count - 1, lap, so_far)


def expand(x):
    lead = x.shape[:-1]
    width = x.shape[-1]
    ones = jnp.ones(lead + (1,), jnp.float32)
    upper, lower = np.triu_indices(width)
    weight = np.where(upper == lower, 0.5**0.5, 1.0).astype(np.float32)
    quad = x[..., upper] * x[..., lower] * weight
    return jnp.concatenate([ones, x, quad], axis=-1)


def add_states(earlier, later):
    return earlier + later


def body(hidden_states, feature_q, feature_k, value_w, window_q, window_k, norm_gain):
    rows = hidden_states.shape[0]
    heads = feature_q.shape[1] // FK
    offset = lax.axis_index("seq") * rows
    whole = lax.all_gather(hidden_states, "head", axis=1, tiled=True)
    query = (jnp.dot(whole, feature_q, preferred_element_type=jnp.float32) * FK ** (-0.25)).reshape(
        rows, heads, FK
    )
    key = (jnp.dot(whole, feature_k, preferred_element_type=jnp.float32) * FK ** (-0.25)).reshape(
        rows, heads, FK
    )
    wquery = jnp.dot(whole, window_q, preferred_element_type=jnp.float32).astype(jnp.bfloat16)
    wkey = jnp.dot(whole, window_k, preferred_element_type=jnp.float32).astype(jnp.bfloat16)
    values_ext = jnp.dot(whole, value_w, preferred_element_type=jnp.float32).astype(jnp.bfloat16)
    prev_keys, prev_values = from_behind((wkey[rows - WIN :], values_ext[rows - WIN :]), "seq", 1)
    key_rows_full = jnp.concatenate([prev_keys, wkey], axis=0)
    values_all = jnp.concatenate([prev_values, values_ext], axis=0)
    value3 = values_ext.reshape(rows, heads, HV)
    phi_q = expand(query)
    phi_k = expand(key)
    width = phi_k.shape[-1]
    local_state = jnp.einsum(
        "lhf,lhv->fhv", phi_k, value3.astype(jnp.float32), precision=HIGH_ACCURACY
    ).reshape(width, heads * HV)
    prefix = prefix_2(local_state, "seq", add_states, jnp.zeros_like(local_state))
    inner = jnp.einsum("lhf,mhf->hlm", query, key, precision=HIGH_ACCURACY)
    kernel = 1.0 + inner + 0.5 * inner * inner
    index_rows = jnp.arange(rows, dtype=jnp.int32)
    causal = index_rows[:, None] >= index_rows[None, :]
    kernel = jnp.where(causal[None], kernel, 0.0).astype(jnp.bfloat16)
    intra = jnp.einsum("hlm,mhv->lhv", kernel, value3, preferred_element_type=jnp.float32)
    cross = jnp.einsum(
        "lhf,fhv->lhv", phi_q, prefix.reshape(width, heads, HV), precision=HIGH_ACCURACY
    )
    linear = intra + cross
    scale = lax.rsqrt(jnp.mean(linear * linear, axis=-1, keepdims=True) + 1e-05)
    normed = linear * scale * norm_gain.reshape(heads, HV)
    query_weight3 = wquery.reshape(rows, heads, WINDOW_HEAD_SIZE)
    key_tensor3 = key_rows_full.reshape(rows + WIN, heads, WINDOW_HEAD_SIZE)
    window_logits = jnp.einsum(
        "qxo,bxo->xqb", query_weight3, key_tensor3, preferred_element_type=jnp.float32
    ) * WINDOW_HEAD_SIZE ** (-0.5)
    query_pos = offset + index_rows[:, None]
    key_pos = offset - WIN + jnp.arange(rows + WIN, dtype=jnp.int32)[None, :]
    valid = (key_pos <= query_pos) & (key_pos > query_pos - WIN) & (key_pos >= 0)
    window_logits = jnp.where(valid[None], window_logits, -1e30)
    top = jnp.max(window_logits, axis=-1, keepdims=True)
    expw = jnp.exp(window_logits - top)
    weights = (expw / jnp.sum(expw, axis=-1, keepdims=True)).astype(jnp.bfloat16)
    window = jnp.einsum(
        "hlm,mhv->lhv",
        weights,
        values_all.reshape(rows + WIN, heads, HV),
        preferred_element_type=jnp.float32,
    )
    return (normed + window).astype(jnp.bfloat16).reshape(rows, heads * HV)


def solution(mesh):
    in_specs = (
        P("seq", "head"),
        P(None, "head"),
        P(None, "head"),
        P(None, "head"),
        P(None, "head"),
        P(None, "head"),
        P("head"),
    )
    out_specs = P("seq", "head")
    return jax.shard_map(body, mesh=mesh, in_specs=in_specs, out_specs=out_specs, check_vma=False)
```

profile of v0, /device:TPU:0, one launch (start us, length us, event | category | flops | bytes accessed | tf_op | source)
XLA Modules:
  0.0 101.9 jit_solution(2306110077940659043)
XLA Ops:
  6.5 10.4 %all_gather.6 = bf16[256,1536]{1,0:T(8,128)(2,1)S(1)} all-gather(bf16[256,384]{1,0:T(8,128)(2,1)} %param.19), channel_id=1, replica_groups=mesh['seq'=8,'head'=4] {'head'}, dimensions={1}, use_global_device_ids=true | all-gather | bytes 983040 | tf_op jit(solution)/shard_map/all_gather | solution.py:50
  17.0 1.5 %convolution_multiply_fusion = f32[256,96]{0,1:T(8,128)S(1)} fusion(bf16[256,1536]{1,0:T(8,128)(2,1)S(1)} %all_gather.6, bf16[1536,96]{0,1:T(8,128)(2,1)} %param.21), kind=kOutput, calls=%fused_computation.22 | convolution fusion | flops 75522048 | bytes 1179648 | tf_op jit(solution)/shard_map/dot_general | solution.py:54
  18.5 0.0 copy-start.9
  18.5 0.1 copy.42
  18.6 0.5 copy-done.9
  19.1 0.8 gather_fusion
  19.9 0.8 gather_fusion.1
  20.7 1.6 %convolution_multiply_fusion.1 = f32[256,96]{0,1:T(8,128)S(1)} fusion(bf16[256,1536]{1,0:T(8,128)(2,1)} %copy-done.1, bf16[1536,96]{0,1:T(8,128)(2,1)} %param.20), kind=kOutput, calls=%fused_computation.23 | convolution fusion | flops 75522048 | bytes 1179648 | tf_op jit(solution)/shard_map/dot_general | solution.py:51
  22.3 0.6 copy-done.7
  22.9 0.1 copy.48
  23.0 1.8 %gather_fusion.2 = f32[136,256,6]{1,2,0:T(8,128)} fusion(f32[256,6,16]{0,1,2:T(8,128)S(1)} %copy.48, s32[1024]{0:T(1024)S(1)} %pad_clamp_fusion.1), kind=kCustom, calls=%fused_computation.2 | custom fusion | bytes 1671712 | tf_op jit(solution)/shard_map/gather | solution.py:38
  24.8 1.8 %gather_fusion.3 = f32[136,256,6]{1,2,0:T(8,128)} fusion(f32[256,6,16]{0,1,2:T(8,128)S(1)} %copy.48, s32[1024]{0:T(1024)S(1)} %pad_clamp_fusion), kind=kCustom, calls=%fused_computation.3 | custom fusion | bytes 1671712 | tf_op jit(solution)/shard_map/gather | solution.py:38
  26.6 2.4 %convolution_convert_fusion.2 = bf16[256,384]{1,0:T(8,128)(2,1)} fusion(bf16[256,1536]{1,0:T(8,128)(2,1)} %copy-done.1, bf16[1536,384]{1,0:T(8,128)(2,1)S(1)} %copy-done), kind=kOutput, calls=%fused_computation.20 | convolution fusion | flops 302088192 | bytes 2162688 | tf_op jit(solution)/shard_map/dot_general | solution.py:59
  29.0 1.8 %copy.41 = bf16[256,384]{0,1:T(8,128)(2,1)} copy(bf16[256,384]{1,0:T(8,128)(2,1)} %convolution_convert_fusion.2) | data formatting | bytes 393216 | tf_op jit(solution)/shard_map/convert_element_type | solution.py:59
  30.8 3.5 %fusion.21 = (f32[256,6,136]{0,2,1:T(8,128)}, f32[256,6,136]{0,2,1:T(8,128)S(1)}) fusion(f32[136,256,6]{1,2,0:T(8,128)} %gather_fusion.3, f32[136,256,6]{1,2,0:T(8,128)} %gather_fusion.2, f32[136]{0:T(256)S(1)} %copy-done.14, f32[136,256,6]{1,2,0:T(8,128)S(1)} %gather_fusion.1, f32[136,256,6]{1,2,0:T(8,128)S(1)} %gather_fusion), kind=kLoop, calls=%fused_computation.38 | loop fusion | flops 835584 | bytes 5014048 | tf_op jit(solution)/shard_map/mul | solution.py:38
  34.2 0.8 fusion.8
  35.1 0.8 copy.46
  35.9 0.0 all-gather.2.cloned.1.call-update
  35.9 1.8 %convolution_convert_fusion = bf16[256,384]{1,0:T(8,128)(2,1)S(1)} fusion(bf16[256,1536]{1,0:T(8,128)(2,1)S(1)} %copy-done.2, bf16[1536,384]{1,0:T(8,128)(2,1)} %param.24), kind=kOutput, calls=%fused_computation.18 | convolution fusion | flops 302088192 | bytes 2162688 | tf_op jit(solution)/shard_map/dot_general | solution.py:58
  37.8 3.6 %collective-permute-start.1 = (bf16[64,384]{1,0:T(8,128)(2,1)S(1)}, bf16[64,384]{1,0:T(8,128)(2,1)S(1)}, u32[]{:S(2)}, u32[]{:S(2)}) collective-permute-start(bf16[64,384]{1,0:T(8,128)(2,1)S(1)} %slice.17), channel_id=1, source_target_pairs={{0,4},{4,8},{8,12},{12,16},{16,20},{20,24},{24,28},{1,5},{5,9},{9,... | collective-permute-start | bytes 147464 | tf_op jit(solution)/shard_map/ppermute | solution.py:17
  41.4 4.0 %collective-permute-start = (bf16[64,384]{1,0:T(8,128)(2,1)S(1)}, bf16[64,384]{1,0:T(8,128)(2,1)}, u32[]{:S(2)}, u32[]{:S(2)}) collective-permute-start(bf16[64,384]{1,0:T(8,128)(2,1)S(1)} %slice.16), channel_id=1, source_target_pairs={{0,4},{4,8},{8,12},{12,16},{16,20},{20,24},{24,28},{1,5},{5,9},{9,... | collective-permute-start | bytes 147464 | tf_op jit(solution)/shard_map/ppermute | solution.py:17
  45.5 0.0 copy-start.17
  45.5 1.7 %fusion.4 = bf16[6,256,256]{2,1,0:T(8,128)(2,1)S(1)} fusion(f32[256,6,16]{0,2,1:T(8,128)S(1)} %bitcast.52, f32[256,6,16]{0,2,1:T(8,128)S(1)} %bitcast.56, pred[256,256]{1,0:T(8,128)(4,1)S(1)} %iota_compare_fusion), kind=kOutput, calls=%fused_computation.13 | convolution fusion | flops 77856768 | bytes 1048576 | tf_op jit(solution)/shard_map/lhf,mhf->hlm/dot_general | solution.py:71
  47.2 0.4 fusion.33
  47.6 0.0 copy-start.13
  47.6 0.6 convolution_convert_fusion.1
  48.2 0.2 and_and_fusion
  48.3 0.1 copy.53
  48.5 0.1 mul.81
  48.6 0.0 collective-permute-done.1
  48.6 0.2 copy.54
  48.8 0.8 pad_maximum_fusion
  49.7 0.2 copy.52
  49.9 2.1 %fusion.32 = (f32[6,256]{1,0:T(8,128)S(1)}, f32[6,256,320]{1,2,0:T(8,128)}) fusion(pred[256,320]{0,1:T(8,128)(4,1)S(1)} %and_and_fusion, bf16[256,6,64]{0,2,1:T(8,128)(2,1)S(1)} %bitcast.59, bf16[320,6,64]{0,2,1:T(8,128)(2,1)S(1)} %bitcast.58), kind=kOutput, calls=%fused_computation.61 | convolution fusion | flops 64880960 | bytes 2496512 | tf_op jit(solution)/shard_map/sub | solution.py:93
  51.9 32.9 %all-gather.2.cloned.1.call-done = f32[8,153,384]{2,1,0:T(8,128)} async-done(((f32[1,153,384]{2,1,0:T(8,128)}), f32[8,153,384]{2,1,0:T(8,128)}) %all-gather.2.cloned.1.call-update) | async-done | bytes 1880080 | tf_op jit(solution)/shard_map/all_gather | solution.py:22
  84.8 7.3 %while.14 = (s32[]{:T(128)}, f32[153,384]{1,0:T(8,128)S(1)}, s32[]{:T(128)}, f32[8,153,384]{2,1,0:T(8,128)}, s32[]{:T(128)}, /*index=5*/s32[]{:T(128)}) while((s32[]{:T(128)}, f32[153,384]{1,0:T(8,128)S(1)}, s32[]{:T(128)}, f32[8,153,384]{2,1,0:T(8,128)}, s32[]{:T(128)}, /*index=5*/s32[]{:T(128)}) %tuple.36), condition=%wide.region_1.2_spmd.clone, body=%wide.region_0.1_spmd.clone.sunk | while | flops 176260 | bytes 705117 | solution.py:29
  84.8 1.1 %add_select_fusion.2 = f32[153,384]{1,0:T(8,128)S(1)} fusion(f32[153,384]{1,0:T(8,128)S(1)} %get-tuple-element.148, f32[8,153,384]{2,1,0:T(8,128)} %get-tuple-element.156, s32[]{:T(128)} %get-tuple-element.147, pred[]{:T(512)S(6)} %compare.3, pred[]{:T(512)S(6)} %lt.21), kind=kLoop, calls=%fused_computation.4.clone.1 | loop fusion | flops 176256 | bytes 705030 | tf_op jit(solution)/shard_map/while/body/eval_jaxpr/jit(_where)/select_n | solution.py:27
  85.9 1.0 add_select_fusion.2
  87.0 1.0 add_select_fusion.2
  88.0 1.0 add_select_fusion.2
  89.1 1.0 add_select_fusion.2
  90.1 1.0 add_select_fusion.2
  91.1 1.0 add_select_fusion.2
  92.2 0.2 copy.47
  92.4 0.8 multiply_reduce_fusion
  93.2 0.6 copy-done.18
  93.9 0.3 fusion.7
  94.2 0.8 copy.55
  (46 shorter events, 0.2 us)
Async XLA Ops:
  6.5 20.0 %copy-start = (bf16[1536,384]{1,0:T(8,128)(2,1)S(1)}, bf16[1536,384]{1,0:T(8,128)(2,1)}, u32[]{:S(2)}) copy-start(bf16[1536,384]{1,0:T(8,128)(2,1)} %param.22) | copy-start | bytes 3538948
  6.5 12.0 %copy-start.15 = (s32[136]{0:T(256)S(1)}, s32[136]{0:T(256)}, u32[]{:S(2)}) copy-start(s32[136]{0:T(256)} %constant.74) | copy-start | bytes 1636
  6.5 12.6 %copy-start.16 = (s32[136]{0:T(256)S(1)}, s32[136]{0:T(256)}, u32[]{:S(2)}) copy-start(s32[136]{0:T(256)} %constant.75) | copy-start | bytes 1636
  6.5 78.3 %all-gather.2.cloned.1.call-start = ((), (), s32[]{:S(2)}) async-start(), calls=%async_computation | async-start | bytes 2211840 | tf_op jit(solution)/shard_map/all_gather | solution.py:22
  17.0 1.6 %copy-start.1 = (bf16[256,1536]{1,0:T(8,128)(2,1)}, bf16[256,1536]{1,0:T(8,128)(2,1)S(1)}, u32[]{:S(2)}) copy-start(bf16[256,1536]{1,0:T(8,128)(2,1)S(1)} %all_gather.6) | copy-start | bytes 2359300
  18.5 0.6 copy-start.9
  22.3 0.6 copy-start.7
  26.6 4.2 %copy-start.14 = (f32[136]{0:T(256)S(1)}, f32[136]{0:T(256)}, u32[]{:S(2)}) copy-start(f32[136]{0:T(256)} %constant.71.clone) | copy-start | bytes 1636
  30.7 3.5 %copy-start.11 = (f32[153]{0:T(256)}, f32[153]{0:T(256)S(1)}, u32[]{:S(2)}) copy-start(f32[153]{0:T(256)S(1)} %pad.7.clone) | copy-start | bytes 1840
  30.7 3.5 %copy-start.4 = (bf16[256,384]{0,1:T(8,128)(2,1)S(1)}, bf16[256,384]{0,1:T(8,128)(2,1)}, u32[]{:S(2)}) copy-start(bf16[256,384]{0,1:T(8,128)(2,1)} %copy.41) | copy-start | bytes 589828
  30.7 3.5 %copy-start.10 = (f32[256,96]{0,1:T(8,128)S(1)}, f32[256,96]{0,1:T(8,128)}, u32[]{:S(2)}) copy-start(f32[256,96]{0,1:T(8,128)} %copy-done.9) | copy-start | bytes 294916
  34.2 1.7 %copy-start.2 = (bf16[256,1536]{1,0:T(8,128)(2,1)S(1)}, bf16[256,1536]{1,0:T(8,128)(2,1)}, u32[]{:S(2)}) copy-start(bf16[256,1536]{1,0:T(8,128)(2,1)} %copy-done.1) | copy-start | bytes 2359300
  35.0 6.3 %copy-start.6 = (bf16[256,384]{1,0:T(8,128)(2,1)S(1)}, bf16[256,384]{1,0:T(8,128)(2,1)}, u32[]{:S(2)}) copy-start(bf16[256,384]{1,0:T(8,128)(2,1)} %convolution_convert_fusion.2) | copy-start | bytes 589828
  35.1 10.4 %copy-start.8 = (f32[256,96]{0,1:T(8,128)S(1)}, f32[256,96]{0,1:T(8,128)}, u32[]{:S(2)}) copy-start(f32[256,96]{0,1:T(8,128)} %copy-done.7) | copy-start | bytes 294916
  37.8 9.4 %copy-start.5 = (bf16[256,384]{0,1:T(8,128)(2,1)S(1)}, bf16[256,384]{0,1:T(8,128)(2,1)}, u32[]{:S(2)}) copy-start(bf16[256,384]{0,1:T(8,128)(2,1)} %copy.41) | copy-start | bytes 589828
  37.8 10.7 %collective-permute-start.1 = (bf16[64,384]{1,0:T(8,128)(2,1)S(1)}, bf16[64,384]{1,0:T(8,128)(2,1)S(1)}, u32[]{:S(2)}, u32[]{:S(2)}) collective-permute-start(bf16[64,384]{1,0:T(8,128)(2,1)S(1)} %slice.17), channel_id=1, source_target_pairs={{0,4},{4,8},{8,12},{12,16},{16,20},{20,24},{24,28},{1,5},{5,9},{9,... | collective-permute-start | bytes 147464 | tf_op jit(solution)/shard_map/ppermute | solution.py:17
  41.4 7.4 %collective-permute-start = (bf16[64,384]{1,0:T(8,128)(2,1)S(1)}, bf16[64,384]{1,0:T(8,128)(2,1)}, u32[]{:S(2)}, u32[]{:S(2)}) collective-permute-start(bf16[64,384]{1,0:T(8,128)(2,1)S(1)} %slice.16), channel_id=1, source_target_pairs={{0,4},{4,8},{8,12},{12,16},{16,20},{20,24},{24,28},{1,5},{5,9},{9,... | collective-permute-start | bytes 147464 | tf_op jit(solution)/shard_map/ppermute | solution.py:17
  45.5 2.1 %copy-start.17 = (bf16[1536,384]{1,0:T(8,128)(2,1)S(1)}, bf16[1536,384]{1,0:T(8,128)(2,1)}, u32[]{:S(2)}) copy-start(bf16[1536,384]{1,0:T(8,128)(2,1)} %param.23) | copy-start | bytes 3538948
  47.6 0.9 copy-start.13
  84.8 7.5 %copy-start.3 = (f32[256,6,136]{0,2,1:T(8,128)S(1)}, f32[256,6,136]{0,2,1:T(8,128)}, u32[]{:S(2)}) copy-start(f32[256,6,136]{0,2,1:T(8,128)} %get-tuple-element.108) | copy-start | bytes 2506756
  84.8 7.5 %copy-start.12 = (f32[153]{0:T(256)S(1)}, f32[153]{0:T(256)}, u32[]{:S(2)}) copy-start(f32[153]{0:T(256)} %copy-done.11) | copy-start | bytes 1840
  92.3 1.5 %copy-start.18 = (f32[6,256,320]{1,2,0:T(8,128)S(1)}, f32[6,256,320]{1,2,0:T(8,128)}, u32[]{:S(2)}) copy-start(f32[6,256,320]{1,2,0:T(8,128)} %get-tuple-element.111) | copy-start | bytes 5898244
Sparse Core Ops, SparseCore 0:
  36.1 48.7 all-gather.1
where the time goes:
time: 102 us
  waiting for transfers between devices  32.9 us (32%)
  matrix products  14 us (14%)
  between operations  13.8 us (14%)
  other arithmetic  11.7 us (11%)
  local copies, waits for them, and re-layouts  11.4 us (11%)
  blocking collectives  10.4 us (10%)
  starting transfers between devices  7.6 us (7%)
    all_gather x1, waiting for transfers between devices, prefix_2(): pieces = lax.all_gather(value, axis)  32.9 us
    all_gather x1, blocking collectives, body(): whole = lax.all_gather(hidden_states, 'head', axis=1, tiled=True)  10.4 us
    ppermute x2, starting transfers between devices, from_behind(): return lax.ppermute(shard, axis, pairs)  7.6 us
    select_n x7, other arithmetic, lap(): return jnp.where(position < mine, longer, so_far)  7.18 us
    gather x4, local copies, waits for them, and re-layouts, expand(): quad = x[..., upper] * x[..., lower] * weight  5.12 us
    mul x1, other arithmetic, expand(): quad = x[..., upper] * x[..., lower] * weight  3.47 us
    dot_general x1, matrix products, body(): jnp.dot(whole, value_w, preferred_element_type=jnp.float32)  2.4 us
    sub x1, matrix products, body(): expw = jnp.exp(window_logits - top)  2.07 us
  transfers between devices with their start and end apart: 3, of which 1 were waited for; matrix products, arithmetic and copies ran while one was open for 8% of the time, Pallas kernels for 0%

commit v1 on v0

--- a/solution.py
+++ b/solution.py
@@ -3,6 +3,7 @@
 import numpy as np
 from jax import lax
 from jax.sharding import PartitionSpec as P
+from jax.lax import all_gather
 
 FK = 16
 HV = 64
@@ -47,7 +48,10 @@
     rows = hidden_states.shape[0]
     heads = feature_q.shape[1] // FK
     offset = lax.axis_index("seq") * rows
-    whole = lax.all_gather(hidden_states, "head", axis=1, tiled=True)
+    group_chains = lambda array_in, row_axis: jnp.concatenate(
+        all_gather(array_in, axis_name=row_axis), axis=1
+    )
+    whole = group_chains(hidden_states, "head")
     query = (jnp.dot(whole, feature_q, preferred_element_type=jnp.float32) * FK ** (-0.25)).reshape(
         rows, heads, FK
     )

time: 102 us -> 98.4 us (0.965)
  matrix products: 14 us -> 9.71 us
  other arithmetic: 11.7 us -> 12.8 us
    dot_general x1, matrix products: 2.4 us -> 0.6 us  [body(): jnp.dot(whole, value_w, preferred_element_type=jnp.float32)]
    convert_element_type x1, local copies, waits for them, and re-layouts: 1.75 us -> 0.15 us  [body(): jnp.dot(whole, value_w, preferred_element_type=jnp.float32)]
    dot_general x1, matrix products: 1.57 us -> 0.27 us  [body(): jnp.dot(whole, feature_q, preferred_element_type=jnp.float32)]
    dot_general x1, matrix products: 1.52 us -> 0.27 us  [body(): jnp.dot(whole, feature_k, preferred_element_type=jnp.float32)]
  transfers between devices with their start and end apart: 3 -> 3, of which waited for: 1 -> 1; matrix products, arithmetic and copies ran while one was open for 8% -> 10% of each run, Pallas kernels for 0% -> 0%
where the time goes in v1:
time: 98.4 us; the launch traced here: 97.8 us
  waiting for transfers between devices  31.9 us (32%)
  between operations  13.7 us (14%)
  other arithmetic  12.8 us (13%)
  local copies, waits for them, and re-layouts  11.7 us (12%)
  blocking collectives  10.4 us (11%)
  matrix products  9.71 us (10%)
  starting transfers between devices  7.46 us (8%)
    all_gather x1, waiting for transfers between devices, prefix_2(): pieces = lax.all_gather(value, axis)  31.9 us
    all_gather x1, blocking collectives, body(): all_gather(array_in, axis_name=row_axis)  10.4 us
    ppermute x2, starting transfers between devices, from_behind(): return lax.ppermute(shard, axis, pairs)  7.46 us
    select_n x7, other arithmetic, lap(): return jnp.where(position < mine, longer, so_far)  7.19 us
    gather x4, local copies, waits for them, and re-layouts, expand(): quad = x[..., upper] * x[..., lower] * weight  6.14 us
    mul x1, other arithmetic, expand(): quad = x[..., upper] * x[..., lower] * weight  3.79 us
    sub x1, matrix products, body(): expw = jnp.exp(window_logits - top)  2.07 us
  transfers between devices with their start and end apart: 3, of which 1 were waited for; matrix products, arithmetic and copies ran while one was open for 10% of the time, Pallas kernels for 0%

profile of v1, /device:TPU:0, one launch (start us, length us, event | category | flops | bytes accessed | tf_op | source)
XLA Modules:
  0.0 97.8 jit_solution(8925416471909589476)
XLA Ops:
  6.5 10.4 %all-gather = bf16[1024,384]{1,0:T(8,128)(2,1)S(1)} all-gather(bf16[256,384]{1,0:T(8,128)(2,1)} %param.19), channel_id=2, replica_groups=mesh['seq'=8,'head'=4] {'head'}, dimensions={0}, use_global_device_ids=true | all-gather | bytes 983040 | tf_op jit(solution)/shard_map/all_gather | solution.py:52
  16.9 0.3 copy.57
  17.2 0.3 convolution_multiply_fusion
  17.5 0.1 copy.59
  17.6 0.0 copy-done.13
  17.6 0.5 copy-done.6
  18.2 0.8 gather_fusion
  19.0 1.8 %gather_fusion.1 = f32[136,256,6]{1,2,0:T(8,128)} fusion(f32[256,6,16]{0,1,2:T(8,128)S(1)} %copy.59, s32[1024]{0:T(1024)S(1)} %pad_clamp_fusion), kind=kCustom, calls=%fused_computation.1 | custom fusion | bytes 1671712 | tf_op jit(solution)/shard_map/gather | solution.py:39
  20.7 0.3 convolution_multiply_fusion.1
  21.0 0.6 copy-done.3
  21.7 0.1 copy.65
  21.7 1.8 %gather_fusion.2 = f32[136,256,6]{1,2,0:T(8,128)} fusion(f32[256,6,16]{0,1,2:T(8,128)S(1)} %copy.65, s32[1024]{0:T(1024)S(1)} %pad_clamp_fusion.1), kind=kCustom, calls=%fused_computation.2 | custom fusion | bytes 1671712 | tf_op jit(solution)/shard_map/gather | solution.py:39
  23.5 1.8 %gather_fusion.3 = f32[136,256,6]{1,2,0:T(8,128)} fusion(f32[256,6,16]{0,1,2:T(8,128)S(1)} %copy.65, s32[1024]{0:T(1024)S(1)} %pad_clamp_fusion), kind=kCustom, calls=%fused_computation.3 | custom fusion | bytes 1671712 | tf_op jit(solution)/shard_map/gather | solution.py:39
  25.3 0.6 convolution_convert_fusion.2
  25.9 0.1 copy.58
  26.1 3.8 %fusion.21 = (f32[256,6,136]{0,2,1:T(8,128)}, f32[256,6,136]{0,2,1:T(8,128)S(1)}) fusion(f32[136,256,6]{1,2,0:T(8,128)} %gather_fusion.3, f32[136,256,6]{1,2,0:T(8,128)} %gather_fusion.2, f32[136]{0:T(256)S(1)} %copy-done.12, f32[136,256,6]{1,2,0:T(8,128)} %gather_fusion.1, f32[136,256,6]{1,2,0:T(8,128)S(1)} %gather_fusion), kind=kLoop, calls=%fused_computation.38 | loop fusion | flops 835584 | bytes 5014048 | tf_op jit(solution)/shard_map/mul | solution.py:39
  29.9 0.8 fusion.8
  30.7 0.9 copy.63
  31.6 0.0 all-gather.3.cloned.1.call-update
  31.6 1.9 %convolution_convert_fusion = bf16[256,384]{1,0:T(8,128)(2,1)S(1)} fusion(bf16[256,1536]{0,1:T(8,128)(2,1)S(1)} %bitcast.54, bf16[1536,384]{1,0:T(8,128)(2,1)} %param.24), kind=kOutput, calls=%fused_computation.18 | convolution fusion | flops 302088192 | bytes 2162688 | tf_op jit(solution)/shard_map/dot_general | solution.py:62
  33.5 0.6 slice.17
  34.1 4.0 %collective-permute-start.1 = (bf16[64,384]{1,0:T(8,128)(2,1)}, bf16[64,384]{1,0:T(8,128)(2,1)}, u32[]{:S(2)}, u32[]{:S(2)}) collective-permute-start(bf16[64,384]{1,0:T(8,128)(2,1)} %slice.17), channel_id=1, source_target_pairs={{0,4},{4,8},{8,12},{12,16},{16,20},{20,24},{24,28},{1,5},{5,9},{9,... | collective-permute-start | bytes 147464 | tf_op jit(solution)/shard_map/ppermute | solution.py:18
  38.1 3.4 %collective-permute-start = (bf16[64,384]{1,0:T(8,128)(2,1)S(1)}, bf16[64,384]{1,0:T(8,128)(2,1)}, u32[]{:S(2)}, u32[]{:S(2)}) collective-permute-start(bf16[64,384]{1,0:T(8,128)(2,1)S(1)} %slice.16), channel_id=1, source_target_pairs={{0,4},{4,8},{8,12},{12,16},{16,20},{20,24},{24,28},{1,5},{5,9},{9,... | collective-permute-start | bytes 147464 | tf_op jit(solution)/shard_map/ppermute | solution.py:18
  41.6 1.7 %fusion.4 = bf16[6,256,256]{2,1,0:T(8,128)(2,1)S(1)} fusion(f32[256,6,16]{0,2,1:T(8,128)S(1)} %bitcast.62, f32[256,6,16]{0,2,1:T(8,128)S(1)} %bitcast.66, pred[256,256]{1,0:T(8,128)(4,1)S(1)} %iota_compare_fusion), kind=kOutput, calls=%fused_computation.13 | convolution fusion | flops 77856768 | bytes 1048576 | tf_op jit(solution)/shard_map/lhf,mhf->hlm/dot_general | solution.py:75
  43.3 0.4 fusion.33
  43.7 0.6 convolution_convert_fusion.1
  44.3 0.2 and_and_fusion
  44.5 0.1 copy.70
  44.6 0.1 mul.81
  44.7 0.8 pad_maximum_fusion.1
  45.5 0.2 copy.71
  45.8 0.8 pad_maximum_fusion
  46.6 0.2 copy.69
  46.8 2.1 %fusion.32 = (f32[6,256]{1,0:T(8,128)S(1)}, f32[6,256,320]{1,2,0:T(8,128)}) fusion(pred[256,320]{0,1:T(8,128)(4,1)S(1)} %and_and_fusion, bf16[256,6,64]{0,2,1:T(8,128)(2,1)S(1)} %bitcast.69, bf16[320,6,64]{0,2,1:T(8,128)(2,1)S(1)} %bitcast.68), kind=kOutput, calls=%fused_computation.61 | convolution fusion | flops 64880960 | bytes 2496512 | tf_op jit(solution)/shard_map/sub | solution.py:97
  48.9 31.9 %all-gather.3.cloned.1.call-done = f32[8,153,384]{2,1,0:T(8,128)} async-done(((f32[1,153,384]{2,1,0:T(8,128)}), f32[8,153,384]{2,1,0:T(8,128)}) %all-gather.3.cloned.1.call-update) | async-done | bytes 1880080 | tf_op jit(solution)/shard_map/all_gather | solution.py:23
  80.8 7.3 %while.14 = (s32[]{:T(128)}, f32[153,384]{1,0:T(8,128)S(1)}, s32[]{:T(128)}, f32[8,153,384]{2,1,0:T(8,128)}, s32[]{:T(128)}, /*index=5*/s32[]{:T(128)}) while((s32[]{:T(128)}, f32[153,384]{1,0:T(8,128)S(1)}, s32[]{:T(128)}, f32[8,153,384]{2,1,0:T(8,128)}, s32[]{:T(128)}, /*index=5*/s32[]{:T(128)}) %tuple.36), condition=%wide.region_1.2_spmd.clone, body=%wide.region_0.1_spmd.clone.sunk | while | flops 176260 | bytes 705117 | solution.py:30
  80.8 1.1 %add_select_fusion.2 = f32[153,384]{1,0:T(8,128)S(1)} fusion(f32[153,384]{1,0:T(8,128)S(1)} %get-tuple-element.148, f32[8,153,384]{2,1,0:T(8,128)} %get-tuple-element.156, s32[]{:T(128)} %get-tuple-element.147, pred[]{:T(512)S(6)} %compare.3, pred[]{:T(512)S(6)} %lt.21), kind=kLoop, calls=%fused_computation.4.clone.1 | loop fusion | flops 176256 | bytes 705030 | tf_op jit(solution)/shard_map/while/body/eval_jaxpr/jit(_where)/select_n | solution.py:28
  81.9 1.0 %add_select_fusion.2 = f32[153,384]{1,0:T(8,128)S(1)} fusion(f32[153,384]{1,0:T(8,128)S(1)} %get-tuple-element.148, f32[8,153,384]{2,1,0:T(8,128)} %get-tuple-element.156, s32[]{:T(128)} %get-tuple-element.147, pred[]{:T(512)S(6)} %compare.3, pred[]{:T(512)S(6)} %lt.21), kind=kLoop, calls=%fused_computation.4.clone.1 | loop fusion | flops 176256 | bytes 705030 | tf_op jit(solution)/shard_map/while/body/eval_jaxpr/jit(_where)/select_n | solution.py:28
  82.9 1.0 %add_select_fusion.2 = f32[153,384]{1,0:T(8,128)S(1)} fusion(f32[153,384]{1,0:T(8,128)S(1)} %get-tuple-element.148, f32[8,153,384]{2,1,0:T(8,128)} %get-tuple-element.156, s32[]{:T(128)} %get-tuple-element.147, pred[]{:T(512)S(6)} %compare.3, pred[]{:T(512)S(6)} %lt.21), kind=kLoop, calls=%fused_computation.4.clone.1 | loop fusion | flops 176256 | bytes 705030 | tf_op jit(solution)/shard_map/while/body/eval_jaxpr/jit(_where)/select_n | solution.py:28
  84.0 1.0 %add_select_fusion.2 = f32[153,384]{1,0:T(8,128)S(1)} fusion(f32[153,384]{1,0:T(8,128)S(1)} %get-tuple-element.148, f32[8,153,384]{2,1,0:T(8,128)} %get-tuple-element.156, s32[]{:T(128)} %get-tuple-element.147, pred[]{:T(512)S(6)} %compare.3, pred[]{:T(512)S(6)} %lt.21), kind=kLoop, calls=%fused_computation.4.clone.1 | loop fusion | flops 176256 | bytes 705030 | tf_op jit(solution)/shard_map/while/body/eval_jaxpr/jit(_where)/select_n | solution.py:28
  85.0 1.0 %add_select_fusion.2 = f32[153,384]{1,0:T(8,128)S(1)} fusion(f32[153,384]{1,0:T(8,128)S(1)} %get-tuple-element.148, f32[8,153,384]{2,1,0:T(8,128)} %get-tuple-element.156, s32[]{:T(128)} %get-tuple-element.147, pred[]{:T(512)S(6)} %compare.3, pred[]{:T(512)S(6)} %lt.21), kind=kLoop, calls=%fused_computation.4.clone.1 | loop fusion | flops 176256 | bytes 705030 | tf_op jit(solution)/shard_map/while/body/eval_jaxpr/jit(_where)/select_n | solution.py:28
  86.0 1.0 %add_select_fusion.2 = f32[153,384]{1,0:T(8,128)S(1)} fusion(f32[153,384]{1,0:T(8,128)S(1)} %get-tuple-element.148, f32[8,153,384]{2,1,0:T(8,128)} %get-tuple-element.156, s32[]{:T(128)} %get-tuple-element.147, pred[]{:T(512)S(6)} %compare.3, pred[]{:T(512)S(6)} %lt.21), kind=kLoop, calls=%fused_computation.4.clone.1 | loop fusion | flops 176256 | bytes 705030 | tf_op jit(solution)/shard_map/while/body/eval_jaxpr/jit(_where)/select_n | solution.py:28
  87.1 1.0 %add_select_fusion.2 = f32[153,384]{1,0:T(8,128)S(1)} fusion(f32[153,384]{1,0:T(8,128)S(1)} %get-tuple-element.148, f32[8,153,384]{2,1,0:T(8,128)} %get-tuple-element.156, s32[]{:T(128)} %get-tuple-element.147, pred[]{:T(512)S(6)} %compare.3, pred[]{:T(512)S(6)} %lt.21), kind=kLoop, calls=%fused_computation.4.clone.1 | loop fusion | flops 176256 | bytes 705030 | tf_op jit(solution)/shard_map/while/body/eval_jaxpr/jit(_where)/select_n | solution.py:28
  88.1 0.2 copy.64
  88.3 0.9 multiply_reduce_fusion
  89.2 0.6 copy-done.15
  89.8 0.3 fusion.7
  90.2 0.8 copy.72
  (41 shorter events, 0.1 us)
Async XLA Ops:
  6.5 18.8 %copy-start = (bf16[1536,384]{1,0:T(8,128)(2,1)S(1)}, bf16[1536,384]{1,0:T(8,128)(2,1)}, u32[]{:S(2)}) copy-start(bf16[1536,384]{1,0:T(8,128)(2,1)} %param.22) | copy-start | bytes 3538948
  6.5 10.7 %copy-start.9 = (bf16[1536,96]{0,1:T(8,128)(2,1)S(1)}, bf16[1536,96]{0,1:T(8,128)(2,1)}, u32[]{:S(2)}) copy-start(bf16[1536,96]{0,1:T(8,128)(2,1)} %param.21) | copy-start | bytes 884740
  6.5 74.2 %all-gather.3.cloned.1.call-start = ((), (), s32[]{:S(2)}) async-start(), calls=%async_computation | async-start | bytes 2211840 | tf_op jit(solution)/shard_map/all_gather | solution.py:23
  16.9 0.7 copy-start.13
  16.9 1.2 %copy-start.14 = (s32[136]{0:T(256)S(1)}, s32[136]{0:T(256)}, u32[]{:S(2)}) copy-start(s32[136]{0:T(256)} %constant.75) | copy-start | bytes 1636
  17.5 0.6 copy-start.6
  18.9 1.8 %copy-start.10 = (bf16[1536,96]{0,1:T(8,128)(2,1)S(1)}, bf16[1536,96]{0,1:T(8,128)(2,1)}, u32[]{:S(2)}) copy-start(bf16[1536,96]{0,1:T(8,128)(2,1)} %param.20) | copy-start | bytes 884740
  21.0 0.6 copy-start.3
  25.3 0.8 copy-start.12
  26.1 3.8 %copy-start.7 = (f32[256,96]{0,1:T(8,128)S(1)}, f32[256,96]{0,1:T(8,128)}, u32[]{:S(2)}) copy-start(f32[256,96]{0,1:T(8,128)} %copy-done.6) | copy-start | bytes 294916
  30.7 10.9 %copy-start.4 = (f32[256,96]{0,1:T(8,128)S(1)}, f32[256,96]{0,1:T(8,128)}, u32[]{:S(2)}) copy-start(f32[256,96]{0,1:T(8,128)} %copy-done.3) | copy-start | bytes 294916
  30.7 10.9 %copy-start.8 = (f32[256,96]{0,1:T(8,128)S(1)}, f32[256,96]{0,1:T(8,128)}, u32[]{:S(2)}) copy-start(f32[256,96]{0,1:T(8,128)} %copy-done.6) | copy-start | bytes 294916
  34.1 10.6 %collective-permute-start.1 = (bf16[64,384]{1,0:T(8,128)(2,1)}, bf16[64,384]{1,0:T(8,128)(2,1)}, u32[]{:S(2)}, u32[]{:S(2)}) collective-permute-start(bf16[64,384]{1,0:T(8,128)(2,1)} %slice.17), channel_id=1, source_target_pairs={{0,4},{4,8},{8,12},{12,16},{16,20},{20,24},{24,28},{1,5},{5,9},{9,... | collective-permute-start | bytes 147464 | tf_op jit(solution)/shard_map/ppermute | solution.py:18
  38.1 7.6 %collective-permute-start = (bf16[64,384]{1,0:T(8,128)(2,1)S(1)}, bf16[64,384]{1,0:T(8,128)(2,1)}, u32[]{:S(2)}, u32[]{:S(2)}) collective-permute-start(bf16[64,384]{1,0:T(8,128)(2,1)S(1)} %slice.16), channel_id=1, source_target_pairs={{0,4},{4,8},{8,12},{12,16},{16,20},{20,24},{24,28},{1,5},{5,9},{9,... | collective-permute-start | bytes 147464 | tf_op jit(solution)/shard_map/ppermute | solution.py:18
  41.6 2.0 %copy-start.2 = (bf16[1536,384]{1,0:T(8,128)(2,1)S(1)}, bf16[1536,384]{1,0:T(8,128)(2,1)}, u32[]{:S(2)}) copy-start(bf16[1536,384]{1,0:T(8,128)(2,1)} %param.23) | copy-start | bytes 3538948
  43.7 0.9 copy-start.11
  80.8 7.5 %copy-start.1 = (f32[256,6,136]{0,2,1:T(8,128)S(1)}, f32[256,6,136]{0,2,1:T(8,128)}, u32[]{:S(2)}) copy-start(f32[256,6,136]{0,2,1:T(8,128)} %get-tuple-element.108) | copy-start | bytes 2506756
  80.8 7.5 %copy-start.5 = (f32[256,96]{0,1:T(8,128)S(1)}, f32[256,96]{0,1:T(8,128)}, u32[]{:S(2)}) copy-start(f32[256,96]{0,1:T(8,128)} %copy-done.3) | copy-start | bytes 294916
  88.3 1.5 %copy-start.15 = (f32[6,256,320]{1,2,0:T(8,128)S(1)}, f32[6,256,320]{1,2,0:T(8,128)}, u32[]{:S(2)}) copy-start(f32[6,256,320]{1,2,0:T(8,128)} %get-tuple-element.111) | copy-start | bytes 5898244
Sparse Core Ops, SparseCore 0:
  31.7 49.0 all-gather.2
